TPU v7x, 512 devices: a whole 4x8x8 slice. The times are simulated.
512 devices in a mesh: actors: 128 (over y, z, core), rep: 4 (over x).
Axes of the slice: x: 4, y: 8, z: 8, core: 2. Of those that a mesh axis runs over, the one named last changes fastest.
Arguments:
- features: bfloat16 [4, 128, 256, 1024], P('rep', 'actors'), may hold values from -6 to 6
- rewards: float32 [4, 128, 256], P('rep', 'actors'), may hold values from -2 to 6, as said below
- lengths: int32 [4, 128, 128], P('rep', 'actors'), may hold values from 1 to 3, 256 in all within a row
- owners: int32 [4, 128, 128], P('rep', 'actors'), may hold values from 0 to 127, each once within a row
- norm_gain: float32 [1024], replicated, may hold values from 0.4 to 1.6
Outputs:
- trainer_rows: bfloat16 [4, 128, 384, 1024], P('rep', 'actors')
- trainer_rewards: float32 [4, 128, 384], P('rep', 'actors')
- trainer_counts: int32 [128], P('actors')
Inputs may be any that keep to these rules, and one draw needn't show every extreme that they name: `rewards`: rewards of each actor are centered on a level that differs from actor to actor.
All inputs are finite; a program needn't handle non-finite values.
Results may differ from a plain program's by a relative error of at most 0.0004.
Values may be sent and summed in bfloat16 or wider, within the bound.
A program may use at most 64 MiB of HBM per device.

v0:
```python
import functools

import jax
import jax.numpy as jnp
from jax import lax
from jax.sharding import Mesh
from jax.sharding import PartitionSpec as P

CAP = 3
ACTORS = ("actors_0", "actors_1", "actors_2")
ACTORS_REP = ("actors_0", "actors_1", "actors_2", "rep")


EPS_NORM = 1e-06
EPS_VAR = 1e-05


def side_by_side(arrays, axis, split_dim, concat_dim, along):
    ends, at = ([], 0)
    for a in arrays[:-1]:
        at += a.shape[along]
        ends.append(at)
    both = jnp.concatenate(arrays, axis=along)
    return tuple(
        jnp.split(
            lax.all_to_all(both, axis, split_axis=split_dim, concat_axis=concat_dim, tiled=True),
            ends,
            axis=along,
        )
    )


def one_axis_at_a_time(x, axes):
    return functools.reduce(lax.psum, axes, x)


def rms_scale(rows, norm_gain):
    widened = rows.astype(jnp.float32)
    square_mean = jnp.mean(widened * widened, axis=-1, keepdims=True)
    return (widened * lax.rsqrt(square_mean + EPS_NORM) * norm_gain).astype(jnp.bfloat16)


def local(features, rewards, lengths, owners, norm_gain):
    rows_here = features[0, 0]
    reward_here = rewards[0, 0]
    game_len = lengths[0, 0]
    game_owner = owners[0, 0]
    games = game_len.shape[0]
    row_count = rows_here.shape[0]
    width = rows_here.shape[1]
    row_total = row_count * lax.axis_size(ACTORS) * lax.axis_size("rep")
    starts = jnp.cumsum(game_len) - game_len
    trainer_ids = jnp.arange(games, dtype=jnp.int32)
    owns_game = (game_owner[None, :] == trainer_ids[:, None]).astype(jnp.int32)
    held_len = jnp.sum(owns_game * game_len[None, :], axis=1)
    held_start = jnp.sum(owns_game * starts[None, :], axis=1)
    slot_pos = jnp.arange(CAP, dtype=jnp.int32)
    usable = slot_pos[None, :] < held_len[:, None]
    row_index = jnp.minimum(held_start[:, None] + slot_pos[None, :], row_count - 1)
    outgoing = jnp.where(
        usable, jnp.take(reward_here, row_index, axis=0), jnp.zeros((), jnp.float32)
    )
    arrived, arrived_len = side_by_side(
        (outgoing, held_len.astype(jnp.float32)[:, None]), ACTORS, 0, 0, 1
    )
    packed = jnp.where(
        usable[:, :, None], jnp.take(rows_here, row_index, axis=0), jnp.zeros((), jnp.bfloat16)
    )
    landed = rms_scale(
        lax.all_to_all(packed, ACTORS, split_axis=0, concat_axis=0, tiled=True), norm_gain=norm_gain
    )
    first, second = (
        one_axis_at_a_time(jnp.sum(arrived), ACTORS_REP),
        one_axis_at_a_time(jnp.sum(arrived * arrived), ACTORS_REP),
    )
    reward_mean = first / row_total
    inv_spread = lax.rsqrt(second / row_total - reward_mean * reward_mean + EPS_VAR)
    keep_slot = slot_pos[None, :].astype(jnp.float32) < arrived_len
    scaled = jnp.where(keep_slot, (arrived - reward_mean) * inv_spread, jnp.zeros((), jnp.float32))
    count_here = jnp.sum(arrived_len).astype(jnp.int32)
    counts = lax.psum(count_here, "rep")
    return (landed.reshape(1, 1, -1, width), scaled.reshape(1, 1, -1), counts.reshape(1))


def solution(mesh):
    finer = Mesh(
        mesh.devices.reshape(8, 8, 2, mesh.shape["rep"]),
        ("actors_0", "actors_1", "actors_2", "rep"),
    )
    return jax.shard_map(
        local,
        mesh=finer,
        in_specs=(
            P("rep", ACTORS, None, None),
            P("rep", ACTORS, None),
            P("rep", ACTORS, None),
            P("rep", ACTORS, None),
            P(),
        ),
        out_specs=(P("rep", ACTORS, None, None), P("rep", ACTORS, None), P(ACTORS)),
        check_vma=False,
    )
```

profile of v0, /device:TPU:1, one launch (start us, length us, event | category | flops | bytes accessed | tf_op | source)
XLA Modules:
  0.0 115.8 jit_solution(7875086391993626325)
XLA Ops:
  0.6 0.0 copy-start
  0.6 0.0 copy-start.1
  0.7 0.8 copy.26
  1.5 0.2 reduce-window.8
  1.7 0.1 reduce
  1.8 0.7 bitcast_subtract_fusion
  2.4 0.8 select_reduce_fusion.1
  3.2 0.1 copy.29
  3.3 0.1 compare_select_fusion
  3.4 0.2 reshape.160
  3.6 0.0 copy-done.1
  3.7 2.8 %gather_fusion.1 = f32[384]{0:T(512)S(1)} fusion(f32[256]{0:T(256)S(1)} %bitcast.16, s32[1024]{0:T(1024)S(1)} %pad_clamp_fusion), kind=kCustom, calls=%fused_computation.1 | custom fusion | bytes 4608 | tf_op jit(solution)/shard_map/jit(_take)/gather | solution.py:61
  6.5 0.2 reshape.167
  6.7 0.1 select_select_fusion.1
  6.8 0.7 pad_maximum_fusion
  7.5 18.4 %all-to-all-start.1 = ((f32[128,1,4]{2,1,0:T(1,128)}), f32[128,1,4]{2,1,0:T(1,128)S(1)}, u32[]{:S(2)}, u32[]{:S(2)}) async-start(f32[128,1,4]{2,1,0:T(1,128)} %bitcast.7), calls=%async_computation.1 | async-start | bytes 131072 | tf_op jit(solution)/shard_map/all_to_all | solution.py:26
  25.9 0.1 iota_compare_fusion.1
  26.0 0.0 copy-done
  26.0 2.1 %gather_fusion = bf16[384,1024]{1,0:T(8,128)(2,1)S(1)} fusion(bf16[256,1024]{1,0:T(8,128)(2,1)S(1)} %bitcast.15, s32[1024]{0:T(1024)S(1)} %pad_clamp_fusion), kind=kCustom, calls=%fused_computation | custom fusion | bytes 1574400 | tf_op jit(solution)/shard_map/jit(_take)/gather | solution.py:67
  28.1 0.5 reshape.159
  28.6 1.7 %select_select_fusion = bf16[128,3,1024]{2,1,0:T(4,128)(2,1)} fusion(bf16[128,3,1024]{2,1,0:T(4,128)(2,1)S(1)} %reshape.159, pred[128,3]{1,0:T(8,128)(4,1)S(1)} %get-tuple-element.18, pred[128,3]{1,0:T(8,128)(4,1)S(1)} %get-tuple-element.17), kind=kLoop, calls=%fused_computation.7 | loop fusion | flops 786432 | bytes 1573632 | tf_op jit(solution)/shard_map/jit(_where)/select_n | solution.py:66
  30.4 7.1 %all-to-all-done.1 = f32[128,1,4]{2,1,0:T(1,128)S(1)} async-done(((f32[128,1,4]{2,1,0:T(1,128)}), f32[128,1,4]{2,1,0:T(1,128)S(1)}, u32[]{:S(2)}, u32[]{:S(2)}) %all-to-all-start.1) | async-done | bytes 2080 | tf_op jit(solution)/shard_map/all_to_all | solution.py:26
  37.4 6.7 %all-to-all-start = ((bf16[128,3,1024]{2,1,0:T(4,128)(2,1)}), bf16[128,3,1024]{2,1,0:T(4,128)(2,1)S(1)}, u32[]{:S(2)}, u32[]{:S(2)}) async-start(bf16[128,3,1024]{2,1,0:T(4,128)(2,1)} %select_select_fusion), calls=%async_computation | async-start | bytes 2097152 | tf_op jit(solution)/shard_map/all_to_all | solution.py:70
  44.1 0.0 copy-start.2
  44.1 0.7 slice_reduce_fusion
  45.5 8.7 %psum.71 = s32[1]{0:T(128)} all-reduce(s32[1]{0:T(128)} %bitcast.9), channel_id=1, replica_groups=mesh['actors_0'=8,'actors_1'=8,'actors_2'=2,'rep'=4] {'rep'}, use_global_device_ids=true, to_apply=%region_15.16 | all-reduce | flops 1 | bytes 8 | tf_op jit(solution)/shard_map/psum | solution.py:81
  54.1 0.6 slice_reduce_fusion.2
  54.8 22.5 %all-reduce.1 = (f32[]{:T(128)}, f32[]{:T(128)}) all-reduce(f32[]{:T(128)} %get-tuple-element.6, f32[]{:T(128)} %get-tuple-element.5), channel_id=1, replica_groups=mesh['actors_0'=8,'actors_1'=8,'actors_2'=2,'rep'=4] {'actors_0'}, use_global_device_ids=true, to_apply=%region_10.11 | all-reduce | flops 2 | bytes 16 | tf_op jit(solution)/shard_map/psum | solution.py:34
  77.3 13.7 %all-reduce = (f32[]{:T(128)}, f32[]{:T(128)}) all-reduce(f32[]{:T(128)} %get-tuple-element.11, f32[]{:T(128)} %get-tuple-element.12), channel_id=1, replica_groups=mesh['actors_0'=8,'actors_1'=8,'actors_2'=2,'rep'=4] {'actors_1'}, use_global_device_ids=true, to_apply=%region_11.12 | all-reduce | flops 2 | bytes 16 | tf_op jit(solution)/shard_map/psum | solution.py:34
  91.0 9.5 %all-reduce.3 = (f32[]{:T(128)}, f32[]{:T(128)}) all-reduce(f32[]{:T(128)} %get-tuple-element.9, f32[]{:T(128)} %get-tuple-element.10), channel_id=1, replica_groups=mesh['actors_0'=8,'actors_1'=8,'actors_2'=2,'rep'=4] {'actors_2'}, use_global_device_ids=true, to_apply=%region_12.13 | all-reduce | flops 2 | bytes 16 | tf_op jit(solution)/shard_map/psum | solution.py:34
  100.5 9.1 %all-reduce.2 = (f32[]{:T(128)}, f32[]{:T(128)}) all-reduce(f32[]{:T(128)} %get-tuple-element.15, f32[]{:T(128)} %get-tuple-element.16), channel_id=1, replica_groups=mesh['actors_0'=8,'actors_1'=8,'actors_2'=2,'rep'=4] {'rep'}, use_global_device_ids=true, to_apply=%region_13.14 | all-reduce | flops 2 | bytes 16 | tf_op jit(solution)/shard_map/psum | solution.py:34
  112.2 0.1 multiply_select_fusion
  112.3 0.8 reshape.156
  113.1 0.0 all-to-all-done
  113.1 0.6 fusion
  113.7 0.0 copy-done.2
  113.7 0.6 fusion.2
  114.3 1.4 %reshape.155 = bf16[1,1,384,1024]{3,2,1,0:T(8,128)(2,1)} reshape(bf16[128,3,1024]{2,1,0:T(4,128)(2,1)S(1)} %fusion.2) | data formatting | bytes 1572864 | tf_op jit(solution)/shard_map/reshape | solution.py:82
  (4 shorter events, 0.0 us)
Async XLA Ops:
  0.6 25.4 %copy-start = (bf16[1,1,256,1024]{3,2,1,0:T(8,128)(2,1)S(1)}, bf16[1,1,256,1024]{3,2,1,0:T(8,128)(2,1)}, u32[]{:S(2)}) copy-start(bf16[1,1,256,1024]{3,2,1,0:T(8,128)(2,1)} %param.5) | copy-start | bytes 1572868
  0.6 3.0 %copy-start.1 = (f32[1,1,256]{2,1,0:T(1,128)S(1)}, f32[1,1,256]{2,1,0:T(1,128)}, u32[]{:S(2)}) copy-start(f32[1,1,256]{2,1,0:T(1,128)} %param.6) | copy-start | bytes 3076
  7.5 29.9 %all-to-all-start.1 = ((f32[128,1,4]{2,1,0:T(1,128)}), f32[128,1,4]{2,1,0:T(1,128)S(1)}, u32[]{:S(2)}, u32[]{:S(2)}) async-start(f32[128,1,4]{2,1,0:T(1,128)} %bitcast.7), calls=%async_computation.1 | async-start | bytes 131072 | tf_op jit(solution)/shard_map/all_to_all | solution.py:26
  37.4 75.6 %all-to-all-start = ((bf16[128,3,1024]{2,1,0:T(4,128)(2,1)}), bf16[128,3,1024]{2,1,0:T(4,128)(2,1)S(1)}, u32[]{:S(2)}, u32[]{:S(2)}) async-start(bf16[128,3,1024]{2,1,0:T(4,128)(2,1)} %select_select_fusion), calls=%async_computation | async-start | bytes 2097152 | tf_op jit(solution)/shard_map/all_to_all | solution.py:70
  44.1 69.6 %copy-start.2 = (f32[1024]{0:T(1024)S(1)}, f32[1024]{0:T(1024)}, u32[]{:S(2)}) copy-start(f32[1024]{0:T(1024)} %param.9) | copy-start | bytes 12292
where the time goes:
time: 116 us
  blocking collectives  63.5 us (55%)
  starting transfers between devices  25.1 us (22%)
  local copies, waits for them, and re-layouts  8.94 us (8%)
  other arithmetic  7.1 us (6%)
  waiting for transfers between devices  7.06 us (6%)
  between operations  4.09 us (4%)
    psum x4, blocking collectives, one_axis_at_a_time(): return functools.reduce(lax.psum, axes, x)  54.8 us
    all_to_all x1, starting transfers between devices, side_by_side(): lax.all_to_all(both, axis, split_axis=split_dim, concat_axis=concat_dim,...  18.4 us
    psum x1, blocking collectives, local(): counts = lax.psum(count_here, 'rep')  8.68 us
    all_to_all x1, waiting for transfers between devices, side_by_side(): lax.all_to_all(both, axis, split_axis=split_dim, concat_axis=concat_dim,...  7.06 us
    all_to_all x1, starting transfers between devices, local(): lax.all_to_all(packed, ACTORS, split_axis=0, concat_axis=0, tiled=True)  6.67 us
    gather x2, local copies, waits for them, and re-layouts, local(): jnp.take(reward_here, row_index, axis=0)  3 us
    gather x2, local copies, waits for them, and re-layouts, local(): jnp.take(rows_here, row_index, axis=0)  2.58 us
  transfers between devices with their start and end apart: 2, of which 1 were waited for; matrix products, arithmetic and copies ran while one was open for 6% of the time, Pallas kernels for 0%

commit v1 on v0

v1 whole, which is shorter than its diff:
```python
import functools

import jax
import jax.numpy as jnp
from jax import lax
from jax.experimental import pallas as pl
from jax.experimental.pallas import tpu as pltpu
from jax.sharding import PartitionSpec as P

CAP = 3
EPS_NORM = 1e-06
EPS_VAR = 1e-05
LANES = 128
VMEM = pl.BlockSpec(memory_space=pltpu.VMEM)
SMEM = pl.BlockSpec(memory_space=pltpu.SMEM)
MESH = pl.DeviceIdType.MESH


def pack_kernel(feats, rews, lens, owns, gain, packed, meta, wide):
    rows, width = feats.shape
    games = lens.shape[1]
    tiles = width // LANES
    length = lens[...].astype(jnp.float32)
    game = lax.broadcasted_iota(jnp.int32, (games, games), 1)
    trainer = lax.broadcasted_iota(jnp.int32, (games, games), 0)
    owned = owns[...] == trainer
    game_of = jnp.sum(jnp.where(owned, game, 0).astype(jnp.float32), axis=1, keepdims=True)
    held_len = jnp.sum(jnp.where(owned, length, 0.0), axis=1, keepdims=True)
    before = game.astype(jnp.float32) < game_of
    held_start = jnp.sum(jnp.where(before, length, 0.0), axis=1, keepdims=True)
    offset = lax.broadcasted_iota(jnp.int32, (games, rows), 1).astype(jnp.float32) - held_start
    usable = offset < held_len

    x = feats[...].astype(jnp.float32)
    square_mean = jnp.mean(x * x, axis=-1, keepdims=True)
    normed = (x * lax.rsqrt(square_mean + EPS_NORM) * gain[...]).astype(jnp.bfloat16)

    reward = rews[...]
    lane = lax.broadcasted_iota(jnp.int32, (games, LANES), 1)
    note = jnp.where(lane == CAP, held_len, 0.0)
    note = jnp.where(lane == CAP + 1, jnp.sum(reward), note)
    note = jnp.where(lane == CAP + 2, jnp.sum(reward * reward), note)
    for j in range(CAP):
        chosen = (offset == float(j)) & usable
        picked = jnp.dot(
            chosen.astype(jnp.float32).astype(jnp.bfloat16), normed, preferred_element_type=jnp.float32
        )
        for t in range(games // 8):
            for c in range(tiles):
                wide[pl.ds(t * 8 * CAP * tiles + j * tiles + c, 8, stride=CAP * tiles), :] = picked[
                    t * 8 : t * 8 + 8, c * LANES : (c + 1) * LANES
                ]
        held = jnp.sum(jnp.where(chosen, reward, 0.0), axis=1, keepdims=True)
        note = jnp.where(lane == j, held, note)
    packed[...] = wide[...].astype(jnp.bfloat16).reshape(packed.shape)
    meta[...] = note.reshape(meta.shape)


def send_kernel(n, n_rep, packed, meta, land, notes, totals, mine, others, m_send, m_recv, b_send, b_recv, s_send, s_recv):
    me = lax.axis_index("actors")
    rep = lax.axis_index("rep")
    barrier = pltpu.get_barrier_semaphore()

    @pl.loop(1, n)
    def _(k):
        pl.semaphore_signal(barrier, inc=1, device_id={"actors": lax.rem(me + k, n)}, device_id_type=MESH)

    for k in range(1, n_rep):
        pl.semaphore_signal(barrier, inc=1, device_id={"rep": lax.rem(rep + k, n_rep)}, device_id_type=MESH)
    pl.semaphore_wait(barrier, n - 1 + n_rep - 1)

    @pl.loop(1, n)
    def _(k):
        peer = lax.rem(me + k, n)
        pltpu.make_async_remote_copy(
            src_ref=meta.at[peer], dst_ref=notes.at[me], send_sem=m_send, recv_sem=m_recv,
            device_id={"actors": peer}, device_id_type=MESH,
        ).start()

    @pl.loop(1, n)
    def _(k):
        peer = lax.rem(me + k, n)
        pltpu.make_async_remote_copy(
            src_ref=packed.at[peer], dst_ref=land.at[me], send_sem=b_send, recv_sem=b_recv,
            device_id={"actors": peer}, device_id_type=MESH,
        ).start()

    notes[me] = meta[me]
    land[me] = packed[me]
    some = pl.ds(0, n - 1)
    pltpu.make_async_copy(notes.at[some], notes.at[some], m_recv).wait()
    total = jnp.sum(notes[...], axis=0)
    mine[...] = total
    copies = []
    for k in range(1, n_rep):
        copies.append(
            pltpu.make_async_remote_copy(
                src_ref=mine, dst_ref=others.at[n_rep - 1 - k], send_sem=s_send.at[k - 1], recv_sem=s_recv.at[n_rep - 1 - k],
                device_id={"rep": lax.rem(rep + k, n_rep)}, device_id_type=MESH,
            )
        )
        copies[-1].start()
    for k in range(n_rep - 1):
        pltpu.make_async_copy(others.at[k], others.at[k], s_recv.at[k]).wait()
    for k in range(n_rep - 1):
        total = total + others[k]
    totals[...] = total
    for copy in copies:
        copy.wait_send()
    pltpu.make_async_copy(notes.at[some], notes.at[some], m_send).wait()
    pltpu.make_async_copy(land.at[some], land.at[some], b_recv).wait()
    pltpu.make_async_copy(land.at[some], land.at[some], b_send).wait()


def unpack_kernel(row_total, land, notes, totals, rows, rews, counts, wide):
    games = land.shape[0]
    slots, width = rows.shape
    tiles = width // LANES
    wide[...] = land[...].reshape(wide.shape).astype(jnp.float32)
    for r in range(slots // 8):
        for c in range(tiles):
            rows[r * 8 : r * 8 + 8, c * LANES : (c + 1) * LANES] = wide[
                pl.ds(r * 8 * tiles + c, 8, stride=tiles), :
            ].astype(jnp.bfloat16)
    total = totals[...]
    counts[0] = jnp.sum(total[0:1, CAP : CAP + 1]).astype(jnp.int32)
    mean = total[0:1, CAP + 1 : CAP + 2] / row_total
    second = total[0:1, CAP + 2 : CAP + 3] / row_total
    spread = lax.rsqrt(second - mean * mean + EPS_VAR)
    note = notes[...]
    slot = lax.broadcasted_iota(jnp.int32, (games, slots), 1) - CAP * lax.broadcasted_iota(jnp.int32, (games, slots), 0)
    out = jnp.zeros((games, slots), jnp.float32)
    for j in range(CAP):
        held = (note[:, j : j + 1] - mean) * spread
        held = jnp.where(float(j) < note[:, CAP : CAP + 1], held, 0.0)
        out = out + jnp.where(slot == j, held, 0.0)
    rews[...] = jnp.sum(out, axis=0, keepdims=True)


def local(n, n_rep, features, rewards, lengths, owners, norm_gain):
    rows, width = features.shape[2:]
    games = lengths.shape[2]
    tiles = width // LANES
    message = (games, CAP * tiles, LANES)
    packed, meta = pl.pallas_call(
        pack_kernel,
        out_shape=(
            jax.ShapeDtypeStruct(message, jnp.bfloat16),
            jax.ShapeDtypeStruct((games, 1, LANES), jnp.float32),
        ),
        in_specs=[VMEM] * 5,
        out_specs=(VMEM, VMEM),
        scratch_shapes=[pltpu.VMEM((games * CAP * tiles, LANES), jnp.float32)],
        name="pack",
    )(features[0, 0], rewards[0], lengths[0], owners[0], norm_gain[None])
    land, notes, totals = pl.pallas_call(
        functools.partial(send_kernel, n, n_rep),
        out_shape=(
            jax.ShapeDtypeStruct(message, jnp.bfloat16),
            jax.ShapeDtypeStruct((games, 1, LANES), jnp.float32),
            jax.ShapeDtypeStruct((1, LANES), jnp.float32),
        ),
        in_specs=[VMEM] * 2,
        out_specs=(VMEM,) * 3,
        scratch_shapes=[
            pltpu.VMEM((1, LANES), jnp.float32),
            pltpu.VMEM((n_rep - 1, 1, LANES), jnp.float32),
            pltpu.SemaphoreType.DMA,
            pltpu.SemaphoreType.DMA,
            pltpu.SemaphoreType.DMA,
            pltpu.SemaphoreType.DMA,
            pltpu.SemaphoreType.DMA((n_rep - 1,)),
            pltpu.SemaphoreType.DMA((n_rep - 1,)),
        ],
        compiler_params=pltpu.CompilerParams(collective_id=0, has_side_effects=True),
        name="send",
    )(packed, meta)
    slots = games * CAP
    landed, scaled, counts = pl.pallas_call(
        functools.partial(unpack_kernel, float(rows * n * n_rep)),
        out_shape=(
            jax.ShapeDtypeStruct((slots, width), jnp.bfloat16),
            jax.ShapeDtypeStruct((1, slots), jnp.float32),
            jax.ShapeDtypeStruct((1,), jnp.int32),
        ),
        in_specs=[VMEM] * 3,
        out_specs=(VMEM, VMEM, SMEM),
        scratch_shapes=[pltpu.VMEM((slots * tiles, LANES), jnp.float32)],
        name="unpack",
    )(land, notes.reshape(games, LANES), totals)
    return landed.reshape(1, 1, slots, width), scaled.reshape(1, 1, slots), counts


def solution(mesh):
    n, n_rep = mesh.shape["actors"], mesh.shape["rep"]
    return jax.shard_map(
        functools.partial(local, n, n_rep),
        mesh=mesh,
        in_specs=(
            P("rep", "actors", None, None),
            P("rep", "actors", None),
            P("rep", "actors", None),
            P("rep", "actors", None),
            P(),
        ),
        out_specs=(P("rep", "actors", None, None), P("rep", "actors", None), P("actors")),
        check_vma=False,
    )
```

time: 116 us -> 49.4 us (0.43)
  blocking collectives: 63.5 us -> 0 us
  Pallas kernels: 0 us -> 48.5 us
  starting transfers between devices: 25.1 us -> 0 us
  local copies, waits for them, and re-layouts: 8.94 us -> 0 us
  other arithmetic: 7.1 us -> 0 us
  waiting for transfers between devices: 7.06 us -> 0 us
  between operations: 4.09 us -> 0.64 us
    psum x5 -> x0, blocking collectives: 63.5 us -> none  [the longest x4 54.8 us: one_axis_at_a_time(): return functools.reduce(lax.psum, axes, x)]
    pallas_call x0 -> x3, Pallas kernels: none -> 48.5 us  [the longest x1 43 us: local(): pl.pallas_call(functools.partial(send_kernel, n, n_rep), out_shape=(jax.S...]
    all_to_all x2 -> x0, starting transfers between devices: 25.1 us -> none  [the longest x1 18.4 us: side_by_side(): lax.all_to_all(both, axis, split_axis=split_dim, concat_axis=concat_dim,...]
    all_to_all x2 -> x0, waiting for transfers between devices: 7.06 us -> none  [the longest x1 7.06 us: side_by_side(): lax.all_to_all(both, axis, split_axis=split_dim, concat_axis=concat_dim,...]
    gather x4 -> x0, local copies, waits for them, and re-layouts: 5.58 us -> none  [the longest x2 3 us: local(): jnp.take(reward_here, row_index, axis=0)]
    reduce_sum x4 -> x0, other arithmetic: 2.69 us -> none  [the longest x1 0.77 us: local(): held_len = jnp.sum(owns_game * game_len[None, :], axis=1)]
    reshape x2 -> x0, local copies, waits for them, and re-layouts: 2.2 us -> none  [the longest x1 1.43 us: local(): landed.reshape(1, 1, -1, width)]
    select_n x4 -> x0, other arithmetic: 2.01 us -> none  [the longest x1 1.73 us: local(): jnp.where(usable[:, :, None], jnp.take(rows_here, row_index, axis=0), jnp...]
  transfers between devices with their start and end apart: 2 -> 0, of which waited for: 1 -> 0; matrix products, arithmetic and copies ran while one was open for 6% -> 0% of each run, Pallas kernels for 0% -> 0%
where the time goes in v1:
time: 49.4 us; the launch traced here: 49.2 us
  Pallas kernels  48.5 us (98%)
  between operations  0.64 us (1%)
    pallas_call x1, Pallas kernels, local(): pl.pallas_call(functools.partial(send_kernel, n, n_rep), out_shape=(jax.S...  43 us
    pallas_call x1, Pallas kernels, local(): pl.pallas_call(functools.partial(unpack_kernel, float(rows * n * n_rep)),...  2.77 us
    pallas_call x1, Pallas kernels, local(): pl.pallas_call(pack_kernel, out_shape=(jax.ShapeDtypeStruct(message, jnp....  2.74 us

profile of v1, /device:TPU:1, one launch (start us, length us, event | category | flops | bytes accessed | tf_op | source)
XLA Modules:
  0.0 49.2 jit_solution(3560340922303027162)
XLA Ops:
  0.6 2.7 %pack.1 = (bf16[128,24,128]{2,1,0:T(8,128)(2,1)}, f32[128,1,128]{2,1,0:T(1,128)}) custom-call(bf16[256,1024]{1,0:T(8,128)(2,1)} %bitcast.8, f32[1,256]{1,0:T(1,128)} %bitcast.11, s32[1,128]{1,0:T(1,128)} %bitcast.12, s32[1,128]{1,0:T(1,128)} %bitcast.13, f32[1,1024]{1,0:T(1,128)} %bitcast.10), custom_call_target="tpu_custom_call" | custom-call | tf_op jit(solution)/shard_map/pack/pallas_call | solution.py:145
  3.4 43.0 %send.1 = (bf16[128,24,128]{2,1,0:T(8,128)(2,1)}, f32[128,1,128]{2,1,0:T(1,128)}, f32[1,128]{1,0:T(1,128)}) custom-call(bf16[128,24,128]{2,1,0:T(8,128)(2,1)} %get-tuple-element.11.packed, f32[128,1,128]{2,1,0:T(1,128)} %get-tuple-element.12.meta), custom_call_target="tpu_custom_call" | custom-call | tf_op jit(solution)/shard_map/send/pallas_call | solution.py:156
  46.4 2.8 %unpack.1 = (bf16[384,1024]{1,0:T(8,128)(2,1)}, f32[1,384]{1,0:T(1,128)}, s32[1]{0:T(128)}) custom-call(bf16[128,24,128]{2,1,0:T(8,128)(2,1)} %get-tuple-element.13.land, f32[128,128]{1,0:T(8,128)} %bitcast.9, f32[1,128]{1,0:T(1,128)} %get-tuple-element.15.totals), custom_call_target="tpu_custom_call" | custom-call | tf_op jit(solution)/shard_map/unpack/pallas_call | solution.py:179

commit v2 on v1

v2 whole, which is shorter than its diff:
```python
import functools

import jax
import jax.numpy as jnp
from jax import lax
from jax.experimental import pallas as pl
from jax.experimental.pallas import tpu as pltpu
from jax.sharding import PartitionSpec as P

CAP = 3
EPS_NORM = 1e-06
EPS_VAR = 1e-05
LANES = 128
SIDE = 8
FIELDS = 16
ORDER = (0, 4, 5, 3, 6, 2, 7, 1)
GROUPS = ((0, 4), (4, 4))
VMEM = pl.BlockSpec(memory_space=pltpu.VMEM)
SMEM = pl.BlockSpec(memory_space=pltpu.SMEM)
HBM = pl.BlockSpec(memory_space=pltpu.HBM)
MESH = pl.DeviceIdType.MESH


def place():
    me = lax.axis_index("actors")
    return me // (2 * SIDE), lax.rem(me // 2, SIDE), lax.rem(me, 2)


def actor(y, z, c):
    return (lax.rem(y, SIDE) * SIDE + lax.rem(z, SIDE)) * 2 + lax.rem(c, 2)


def distance(k):
    out = jnp.zeros_like(k)
    for i, d in enumerate(ORDER):
        out = jnp.where(k == i, d, out)
    return out


def wait(sem, ref):
    pltpu.make_async_copy(ref, ref, sem).wait()


def route_kernel(
    n_rep, row_total, feats_in, rews_in, lens_in, owns_in, gain_in, spread_rows, spread_rews, counts,
    feats, rews, lens, owns, gain, wide, packed, via_z, via_y, land_z, land_y,
    note_z, note_c, notes1, notes2, mine, others,
    in_sem, a_send, b_send, a_recv, b_recv, a2_send, b2_send, a2_recv, b2_recv,
    n1_send, n1_recv, n2_send, n2_recv, s_send, s_recv,
):
    y, z, c = place()
    rep = lax.axis_index("rep")
    tiles = feats.shape[1] // LANES
    piece = CAP * tiles
    rows = feats.shape[0]
    games = lens.shape[1]

    inputs = [
        pltpu.make_async_copy(src, dst, in_sem.at[i])
        for i, (src, dst) in enumerate(
            ((feats_in, feats), (rews_in, rews), (lens_in, lens), (owns_in, owns), (gain_in, gain))
        )
    ]
    for copy in inputs:
        copy.start()
    barrier = pltpu.get_barrier_semaphore()
    for d in ORDER[1:]:
        for peer in (actor(y, z + d, c), actor(y + d, z, c), actor(y, z + d, c + 1)):
            pl.semaphore_signal(barrier, inc=1, device_id={"actors": peer}, device_id_type=MESH)
    pl.semaphore_signal(barrier, inc=1, device_id={"actors": actor(y, z, c + 1)}, device_id_type=MESH)
    for k in range(1, n_rep):
        pl.semaphore_signal(barrier, inc=1, device_id={"rep": lax.rem(rep + k, n_rep)}, device_id_type=MESH)
    for copy in inputs[1:]:
        copy.wait()

    row = lax.broadcasted_iota(jnp.int32, (games, 1), 0)
    inner = row & (SIDE - 1)
    step = distance((row // SIDE) & (SIDE - 1))
    near = row < games // 2
    to_y = jnp.where(near, inner, (y + step) & (SIDE - 1))
    to_z = jnp.where(near, (z + step) & (SIDE - 1), inner)
    trainer = (to_y * SIDE + to_z) * 2 + jnp.where(near, c, 1 - c)
    length = lens[...].astype(jnp.float32)
    game = lax.broadcasted_iota(jnp.int32, (games, games), 1).astype(jnp.float32)
    owned = owns[...] == trainer
    game_of = jnp.sum(jnp.where(owned, game, 0.0), axis=1, keepdims=True)
    held_len = jnp.sum(jnp.where(owned, length, 0.0), axis=1, keepdims=True)
    held_start = jnp.sum(jnp.where(game < game_of, length, 0.0), axis=1, keepdims=True)
    offset = lax.broadcasted_iota(jnp.int32, (games, rows), 1).astype(jnp.float32) - held_start
    usable = offset < held_len

    reward = rews[...]
    lane = lax.broadcasted_iota(jnp.int32, (games, LANES), 1) - to_y * FIELDS
    note = jnp.where(lane == CAP, held_len, 0.0)
    note = jnp.where(lane == CAP + 1, jnp.sum(reward), note)
    note = jnp.where(lane == CAP + 2, jnp.sum(reward * reward), note)
    chosen = []
    for j in range(CAP):
        chosen.append((offset == float(j)) & usable)
        held = jnp.sum(jnp.where(chosen[j], reward, 0.0), axis=1, keepdims=True)
        note = jnp.where(lane == j, held, note)
    crossing = jnp.zeros((SIDE, LANES), jnp.float32)
    for k in range(SIDE):
        note_z[k] = jnp.sum(note[k * SIDE : (k + 1) * SIDE], axis=0, keepdims=True)
        crossing = crossing + note[games // 2 + k * SIDE : games // 2 + (k + 1) * SIDE]
    note_c[...] = crossing.reshape(note_c.shape)

    inputs[0].wait()
    x = feats[...].astype(jnp.float32)
    square_mean = jnp.mean(x * x, axis=-1, keepdims=True)
    normed = (x * lax.rsqrt(square_mean + EPS_NORM) * gain[...]).astype(jnp.bfloat16)
    for j in range(CAP):
        picked = jnp.dot(
            chosen[j].astype(jnp.float32).astype(jnp.bfloat16), normed, preferred_element_type=jnp.float32
        )
        for t in range(games // 8):
            for q in range(tiles):
                wide[pl.ds(t * 8 * piece + j * tiles + q, 8, stride=piece), :] = picked[
                    t * 8 : t * 8 + 8, q * LANES : (q + 1) * LANES
                ]
    packed[...] = wide[...].astype(jnp.bfloat16).reshape(packed.shape)
    via_z[0] = packed[0, 0]
    via_y[0] = packed[1, 0]
    notes1[0] = note_z[0]

    pl.semaphore_wait(barrier, 3 * SIDE - 2 + n_rep - 1)

    def send(src, dst, send_sem, recv_sem, peer):
        pltpu.make_async_remote_copy(
            src_ref=src, dst_ref=dst, send_sem=send_sem, recv_sem=recv_sem, device_id=peer, device_id_type=MESH
        ).start()

    for k in range(SIDE):
        d = ORDER[k]
        if k:
            send(note_z.at[k], notes1.at[k], n1_send, n1_recv, {"actors": actor(y, z + d, c)})
        send(
            note_c.at[lax.rem(z + d, SIDE)], notes1.at[SIDE + k], n1_send, n1_recv,
            {"actors": actor(y, z + d, c + 1)},
        )
    for k in range(1, SIDE):
        d = ORDER[k]
        send(packed.at[0, k], via_z.at[k], a_send, a_recv.at[k], {"actors": actor(y, z + d, c)})
        send(packed.at[1, k], via_y.at[k], b_send, b_recv.at[k], {"actors": actor(y + d, z, c)})

    wait(n1_recv, notes1.at[pl.ds(1, 2 * SIDE - 1)])
    for k in range(1, SIDE):
        send(notes1, notes2.at[k], n2_send, n2_recv, {"actors": actor(y + ORDER[k], z, c)})
    notes2[0] = notes1[...]

    for g, (low, count) in enumerate(GROUPS):
        some = pl.ds(low, count)
        for k in range(max(low, 1), low + count):
            wait(a_recv.at[k], via_z.at[k])
        for k in range(1, SIDE):
            d = ORDER[k]
            send(
                via_z.at[some, lax.rem(y + d, SIDE)], land_z.at[k, some], a2_send, a2_recv.at[k, g],
                {"actors": actor(y + d, z, c)},
            )
        for k in range(max(low, 1), low + count):
            wait(b_recv.at[k], via_y.at[k])
        for k in range(SIDE):
            d = ORDER[k]
            send(
                via_y.at[some, lax.rem(z + d, SIDE)], land_y.at[k, some], b2_send, b2_recv.at[k, g],
                {"actors": actor(y, z + d, c + 1)},
            )

    wait(n2_recv, notes2.at[pl.ds(1, SIDE - 1)])
    arrived = notes2[...].reshape(games, LANES)
    total = jnp.sum(arrived, axis=0, keepdims=True)
    mine[...] = total
    for k in range(1, n_rep):
        send(mine, others.at[k - 1], s_send.at[k - 1], s_recv.at[k - 1], {"rep": lax.rem(rep + k, n_rep)})

    def widen(value, ky, kz, core):
        source = actor(y + SIDE - ORDER[ky], z + SIDE - ORDER[kz], core)
        spread_rows[pl.ds(pl.multiple_of(source * piece, 8), piece), :] = value.astype(jnp.float32)

    for k in range(SIDE):
        widen(via_z[k, y], 0, k, c)

    for k in range(1, n_rep):
        wait(s_recv.at[k - 1], others.at[k - 1])
    for k in range(1, n_rep):
        total = total + others[k - 1]
    row_lane = lax.broadcasted_iota(jnp.int32, (1, LANES), 1) - y * FIELDS

    def field(i):
        return jnp.sum(jnp.where(row_lane == i, total, 0.0), axis=1, keepdims=True)

    counts[...] = jnp.broadcast_to(field(CAP), counts.shape).astype(jnp.int32)
    mean = field(CAP + 1) / row_total
    spread = lax.rsqrt(field(CAP + 2) / row_total - mean * mean + EPS_VAR)
    from_y = (y + SIDE - distance(row // (2 * SIDE))) & (SIDE - 1)
    from_z = (z + SIDE - distance(inner)) & (SIDE - 1)
    source = (from_y * SIDE + from_z) * 2 + jnp.where((row & SIDE) == 0, c, 1 - c)
    slots = games * CAP
    slot = lax.broadcasted_iota(jnp.int32, (games, slots), 1) - CAP * source
    lane = lax.broadcasted_iota(jnp.int32, (games, LANES), 1) - y * FIELDS

    def column(i):
        return jnp.sum(jnp.where(lane == i, arrived, 0.0), axis=1, keepdims=True)

    held_len = column(CAP)
    out = jnp.zeros((games, slots), jnp.float32)
    for j in range(CAP):
        value = jnp.where(float(j) < held_len, (column(j) - mean) * spread, 0.0)
        out = out + jnp.where(slot == j, value, 0.0)
    spread_rews[...] = jnp.sum(out, axis=0, keepdims=True)

    for g, (low, count) in enumerate(GROUPS):
        some = pl.ds(low, count)
        for k in range(SIDE):
            if k:
                wait(a2_recv.at[k, g], land_z.at[k, some])
                for i in range(low, low + count):
                    widen(land_z[k, i], k, i, c)
            wait(b2_recv.at[k, g], land_y.at[k, some])
            for i in range(low, low + count):
                widen(land_y[k, i], i, k, c + 1)

    rest = pl.ds(1, SIDE - 1)
    wait(n1_send, notes1.at[pl.ds(1, 2 * SIDE - 1)])
    wait(n2_send, notes2.at[rest])
    for k in range(1, n_rep):
        wait(s_send.at[k - 1], others.at[k - 1])
    wait(a_send, via_z.at[rest])
    wait(b_send, via_y.at[rest])
    wait(a2_send, land_z.at[rest])
    wait(b2_send, land_y)


def write_kernel(spread_rows, spread_rews, count, rows, rews, counts):
    tiles = rows.shape[1] // LANES
    for r in range(rows.shape[0] // 8):
        for q in range(tiles):
            rows[r * 8 : r * 8 + 8, q * LANES : (q + 1) * LANES] = spread_rows[
                pl.ds(r * 8 * tiles + q, 8, stride=tiles), :
            ].astype(jnp.bfloat16)
    rews[...] = spread_rews[...]
    counts[0] = jnp.max(count[...])


def local(n, n_rep, features, rewards, lengths, owners, norm_gain):
    rows, width = features.shape[2:]
    games = lengths.shape[2]
    piece = CAP * width // LANES
    slots = games * CAP
    DMA = pltpu.SemaphoreType.DMA
    block = pltpu.VMEM((SIDE, SIDE, piece, LANES), jnp.bfloat16)
    spread_rows, spread_rews, count = pl.pallas_call(
        functools.partial(route_kernel, n_rep, float(rows * n * n_rep)),
        out_shape=(
            jax.ShapeDtypeStruct((games * piece, LANES), jnp.float32),
            jax.ShapeDtypeStruct((1, slots), jnp.float32),
            jax.ShapeDtypeStruct((1, LANES), jnp.int32),
        ),
        in_specs=[HBM] * 5,
        out_specs=(VMEM,) * 3,
        scratch_shapes=[
            pltpu.VMEM((rows, width), jnp.bfloat16),
            pltpu.VMEM((1, rows), jnp.float32),
            pltpu.VMEM((1, games), jnp.int32),
            pltpu.VMEM((1, games), jnp.int32),
            pltpu.VMEM((1, width), jnp.float32),
            pltpu.VMEM((games * piece, LANES), jnp.float32),
            pltpu.VMEM((2, SIDE, SIDE, piece, LANES), jnp.bfloat16),
            block,
            block,
            block,
            block,
            pltpu.VMEM((SIDE, 1, LANES), jnp.float32),
            pltpu.VMEM((SIDE, 1, LANES), jnp.float32),
            pltpu.VMEM((2 * SIDE, 1, LANES), jnp.float32),
            pltpu.VMEM((SIDE, 2 * SIDE, 1, LANES), jnp.float32),
            pltpu.VMEM((1, LANES), jnp.float32),
            pltpu.VMEM((n_rep - 1, 1, LANES), jnp.float32),
            DMA((5,)),
            DMA,
            DMA,
            DMA((SIDE,)),
            DMA((SIDE,)),
            DMA,
            DMA,
            DMA((SIDE, len(GROUPS))),
            DMA((SIDE, len(GROUPS))),
            DMA,
            DMA,
            DMA,
            DMA,
            DMA((n_rep - 1,)),
            DMA((n_rep - 1,)),
        ],
        compiler_params=pltpu.CompilerParams(
            collective_id=0, has_side_effects=True, vmem_limit_bytes=24 * 1024 * 1024
        ),
        name="route",
    )(features[0, 0], rewards[0], lengths[0], owners[0], norm_gain[None])
    landed, scaled, counts = pl.pallas_call(
        write_kernel,
        out_shape=(
            jax.ShapeDtypeStruct((slots, width), jnp.bfloat16),
            jax.ShapeDtypeStruct((1, slots), jnp.float32),
            jax.ShapeDtypeStruct((1,), jnp.int32),
        ),
        in_specs=[VMEM] * 3,
        out_specs=(VMEM, VMEM, SMEM),
        compiler_params=pltpu.CompilerParams(vmem_limit_bytes=24 * 1024 * 1024),
        name="write",
    )(spread_rows, spread_rews, count)
    return landed.reshape(1, 1, slots, width), scaled.reshape(1, 1, slots), counts


def solution(mesh):
    n, n_rep = mesh.shape["actors"], mesh.shape["rep"]
    return jax.shard_map(
        functools.partial(local, n, n_rep),
        mesh=mesh,
        in_specs=(
            P("rep", "actors", None, None),
            P("rep", "actors", None),
            P("rep", "actors", None),
            P("rep", "actors", None),
            P(),
        ),
        out_specs=(P("rep", "actors", None, None), P("rep", "actors", None), P("actors")),
        check_vma=False,
    )
```

time: 49.4 us -> 40.6 us (0.82)
  Pallas kernels: 48.5 us -> 36 us
  local copies, waits for them, and re-layouts: 0 us -> 3.71 us
    pallas_call x3 -> x2, Pallas kernels: 48.5 us -> 36 us  [the longest x1 34.8 us: local(): pl.pallas_call(functools.partial(route_kernel, n_rep, float(rows * n * n_...]
    unnamed x0 -> x10, local copies, waits for them, and re-layouts: none -> 3.71 us
where the time goes in v2:
time: 40.6 us; the launch traced here: 40.4 us
  Pallas kernels  36 us (89%)
  local copies, waits for them, and re-layouts  3.71 us (9%)
  between operations  0.65 us (2%)
    pallas_call x1, Pallas kernels, local(): pl.pallas_call(functools.partial(route_kernel, n_rep, float(rows * n * n_...  34.8 us
    unnamed x10, local copies, waits for them, and re-layouts  3.71 us
    pallas_call x1, Pallas kernels, local(): pl.pallas_call(write_kernel, out_shape=(jax.ShapeDtypeStruct((slots, widt...  1.23 us

profile of v2, /device:TPU:1, one launch (start us, length us, event | category | flops | bytes accessed | tf_op | source)
XLA Modules:
  0.0 40.4 jit_solution(6718598193464345414)
XLA Ops:
  0.6 0.0 copy-start
  0.6 1.0 %copy-done = bf16[1,1,256,1024]{3,2,1,0:T(8,128)(2,1)S(1)} copy-done((bf16[1,1,256,1024]{3,2,1,0:T(8,128)(2,1)S(1)}, bf16[1,1,256,1024]{3,2,1,0:T(8,128)(2,1)}, u32[]{:S(2)}) %copy-start) | copy-done | bytes 524312
  1.7 0.0 copy-start.1
  1.7 0.7 %copy-done.1 = f32[1024]{0:T(1024)S(1)} copy-done((f32[1024]{0:T(1024)S(1)}, f32[1024]{0:T(1024)}, u32[]{:S(2)}) %copy-start.1) | copy-done | bytes 4120
  2.4 0.0 copy-start.2
  2.4 0.7 %copy-done.2 = f32[1,1,256]{2,1,0:T(1,128)S(1)} copy-done((f32[1,1,256]{2,1,0:T(1,128)S(1)}, f32[1,1,256]{2,1,0:T(1,128)}, u32[]{:S(2)}) %copy-start.2) | copy-done | bytes 1048
  3.0 0.0 copy-start.3
  3.0 0.7 %copy-done.3 = s32[1,1,128]{2,1,0:T(1,128)S(1)} copy-done((s32[1,1,128]{2,1,0:T(1,128)S(1)}, s32[1,1,128]{2,1,0:T(1,128)}, u32[]{:S(2)}) %copy-start.3) | copy-done | bytes 536
  3.7 0.0 copy-start.4
  3.7 0.7 %copy-done.4 = s32[1,1,128]{2,1,0:T(1,128)S(1)} copy-done((s32[1,1,128]{2,1,0:T(1,128)S(1)}, s32[1,1,128]{2,1,0:T(1,128)}, u32[]{:S(2)}) %copy-start.4) | copy-done | bytes 536
  4.4 34.8 %route.1 = (f32[3072,128]{1,0:T(8,128)S(1)}, f32[1,384]{1,0:T(1,128)S(1)}, s32[1,128]{1,0:T(1,128)S(1)}) custom-call(bf16[256,1024]{1,0:T(8,128)(2,1)S(1)} %bitcast.7, f32[1,256]{1,0:T(1,128)S(1)} %bitcast.9, s32[1,128]{1,0:T(1,128)S(1)} %bitcast.10, s32[1,128]{1,0:T(1,128)S(1)} %bitcast.11, f32[1,1024]{1,0:T(1,128)S(1)} %bitcast.8), custom_call_target="tpu_custom_call" | custom-call | tf_op jit(solution)/shard_map/route/pallas_call | solution.py:253
  39.1 1.2 %write.1 = (bf16[384,1024]{1,0:T(8,128)(2,1)}, f32[1,384]{1,0:T(1,128)}, s32[1]{0:T(128)}) custom-call(f32[3072,128]{1,0:T(8,128)S(1)} %get-tuple-element.9.spread_rows, f32[1,384]{1,0:T(1,128)S(1)} %get-tuple-element.10.spread_rews, s32[1,128]{1,0:T(1,128)S(1)} %get-tuple-element.11.count), custom_call_target="tpu_custom_call" | custom-call | tf_op jit(solution)/shard_map/write/pallas_call | solution.py:301
Async XLA Ops:
  0.6 1.0 %copy-start = (bf16[1,1,256,1024]{3,2,1,0:T(8,128)(2,1)S(1)}, bf16[1,1,256,1024]{3,2,1,0:T(8,128)(2,1)}, u32[]{:S(2)}) copy-start(bf16[1,1,256,1024]{3,2,1,0:T(8,128)(2,1)} %param.5) | copy-start | bytes 1572868
  1.7 0.7 %copy-start.1 = (f32[1024]{0:T(1024)S(1)}, f32[1024]{0:T(1024)}, u32[]{:S(2)}) copy-start(f32[1024]{0:T(1024)} %param.9) | copy-start | bytes 12292
  2.4 0.7 %copy-start.2 = (f32[1,1,256]{2,1,0:T(1,128)S(1)}, f32[1,1,256]{2,1,0:T(1,128)}, u32[]{:S(2)}) copy-start(f32[1,1,256]{2,1,0:T(1,128)} %param.6) | copy-start | bytes 3076
  3.0 0.7 %copy-start.3 = (s32[1,1,128]{2,1,0:T(1,128)S(1)}, s32[1,1,128]{2,1,0:T(1,128)}, u32[]{:S(2)}) copy-start(s32[1,1,128]{2,1,0:T(1,128)} %param.7) | copy-start | bytes 1540
  3.7 0.7 %copy-start.4 = (s32[1,1,128]{2,1,0:T(1,128)S(1)}, s32[1,1,128]{2,1,0:T(1,128)}, u32[]{:S(2)}) copy-start(s32[1,1,128]{2,1,0:T(1,128)} %param.8) | copy-start | bytes 1540

commit v3 on v2

--- a/solution.py
+++ b/solution.py
@@ -12,7 +12,7 @@
 EPS_VAR = 1e-05
 LANES = 128
 SIDE = 8
-FIELDS = 16
+FIELDS = 8
 ORDER = (0, 4, 5, 3, 6, 2, 7, 1)
 GROUPS = ((0, 4), (4, 4))
 VMEM = pl.BlockSpec(memory_space=pltpu.VMEM)
@@ -90,7 +90,8 @@
     usable = offset < held_len
 
     reward = rews[...]
-    lane = lax.broadcasted_iota(jnp.int32, (games, LANES), 1) - to_y * FIELDS
+    half = SIDE * FIELDS
+    lane = lax.broadcasted_iota(jnp.int32, (games, LANES), 1) - to_y * FIELDS - jnp.where(near, 0, half)
     note = jnp.where(lane == CAP, held_len, 0.0)
     note = jnp.where(lane == CAP + 1, jnp.sum(reward), note)
     note = jnp.where(lane == CAP + 2, jnp.sum(reward * reward), note)
@@ -144,9 +145,9 @@
         send(packed.at[1, k], via_y.at[k], b_send, b_recv.at[k], {"actors": actor(y + d, z, c)})
 
     wait(n1_recv, notes1.at[pl.ds(1, 2 * SIDE - 1)])
+    notes2[0] = notes1[0:SIDE] + notes1[SIDE:]
     for k in range(1, SIDE):
-        send(notes1, notes2.at[k], n2_send, n2_recv, {"actors": actor(y + ORDER[k], z, c)})
-    notes2[0] = notes1[...]
+        send(notes2.at[0], notes2.at[k], n2_send, n2_recv, {"actors": actor(y + ORDER[k], z, c)})
 
     for g, (low, count) in enumerate(GROUPS):
         some = pl.ds(low, count)
@@ -168,7 +169,7 @@
             )
 
     wait(n2_recv, notes2.at[pl.ds(1, SIDE - 1)])
-    arrived = notes2[...].reshape(games, LANES)
+    arrived = notes2[...].reshape(SIDE * SIDE, LANES)
     total = jnp.sum(arrived, axis=0, keepdims=True)
     mine[...] = total
     for k in range(1, n_rep):
@@ -188,26 +189,28 @@
     row_lane = lax.broadcasted_iota(jnp.int32, (1, LANES), 1) - y * FIELDS
 
     def field(i):
-        return jnp.sum(jnp.where(row_lane == i, total, 0.0), axis=1, keepdims=True)
+        return jnp.sum(jnp.where((row_lane == i) | (row_lane == i + half), total, 0.0), axis=1, keepdims=True)
 
     counts[...] = jnp.broadcast_to(field(CAP), counts.shape).astype(jnp.int32)
     mean = field(CAP + 1) / row_total
     spread = lax.rsqrt(field(CAP + 2) / row_total - mean * mean + EPS_VAR)
-    from_y = (y + SIDE - distance(row // (2 * SIDE))) & (SIDE - 1)
-    from_z = (z + SIDE - distance(inner)) & (SIDE - 1)
-    source = (from_y * SIDE + from_z) * 2 + jnp.where((row & SIDE) == 0, c, 1 - c)
+    pair = lax.broadcasted_iota(jnp.int32, (SIDE * SIDE, 1), 0)
+    from_y = (y + SIDE - distance(pair // SIDE)) & (SIDE - 1)
+    from_z = (z + SIDE - distance(pair & (SIDE - 1))) & (SIDE - 1)
     slots = games * CAP
-    slot = lax.broadcasted_iota(jnp.int32, (games, slots), 1) - CAP * source
-    lane = lax.broadcasted_iota(jnp.int32, (games, LANES), 1) - y * FIELDS
+    lane = lax.broadcasted_iota(jnp.int32, (SIDE * SIDE, LANES), 1) - y * FIELDS
 
     def column(i):
         return jnp.sum(jnp.where(lane == i, arrived, 0.0), axis=1, keepdims=True)
 
-    held_len = column(CAP)
-    out = jnp.zeros((games, slots), jnp.float32)
-    for j in range(CAP):
-        value = jnp.where(float(j) < held_len, (column(j) - mean) * spread, 0.0)
-        out = out + jnp.where(slot == j, value, 0.0)
+    out = jnp.zeros((SIDE * SIDE, slots), jnp.float32)
+    for h in range(2):
+        source = (from_y * SIDE + from_z) * 2 + jnp.where(h == c, 0, 1)
+        slot = lax.broadcasted_iota(jnp.int32, (SIDE * SIDE, slots), 1) - CAP * source
+        held_len = column(h * half + CAP)
+        for j in range(CAP):
+            value = jnp.where(float(j) < held_len, (column(h * half + j) - mean) * spread, 0.0)
+            out = out + jnp.where(slot == j, value, 0.0)
     spread_rews[...] = jnp.sum(out, axis=0, keepdims=True)
 
     for g, (low, count) in enumerate(GROUPS):
@@ -249,6 +252,7 @@
     piece = CAP * width // LANES
     slots = games * CAP
     DMA = pltpu.SemaphoreType.DMA
+    inputs = (features[0, 0], rewards[0], lengths[0], owners[0], norm_gain[None])
     block = pltpu.VMEM((SIDE, SIDE, piece, LANES), jnp.bfloat16)
     spread_rows, spread_rews, count = pl.pallas_call(
         functools.partial(route_kernel, n_rep, float(rows * n * n_rep)),
@@ -274,7 +278,7 @@
             pltpu.VMEM((SIDE, 1, LANES), jnp.float32),
             pltpu.VMEM((SIDE, 1, LANES), jnp.float32),
             pltpu.VMEM((2 * SIDE, 1, LANES), jnp.float32),
-            pltpu.VMEM((SIDE, 2 * SIDE, 1, LANES), jnp.float32),
+            pltpu.VMEM((SIDE, SIDE, 1, LANES), jnp.float32),
             pltpu.VMEM((1, LANES), jnp.float32),
             pltpu.VMEM((n_rep - 1, 1, LANES), jnp.float32),
             DMA((5,)),
@@ -297,7 +301,7 @@
             collective_id=0, has_side_effects=True, vmem_limit_bytes=24 * 1024 * 1024
         ),
         name="route",
-    )(features[0, 0], rewards[0], lengths[0], owners[0], norm_gain[None])
+    )(*(pltpu.with_memory_space_constraint(a, pltpu.HBM) for a in inputs))
     landed, scaled, counts = pl.pallas_call(
         write_kernel,
         out_shape=(

time: 40.6 us -> 36.7 us (0.904)
  local copies, waits for them, and re-layouts: 3.71 us -> 0 us
    unnamed x10 -> x0, local copies, waits for them, and re-layouts: 3.71 us -> none
where the time goes in v3:
time: 36.7 us; the launch traced here: 36.6 us
  Pallas kernels  36 us (98%)
  between operations  0.64 us (2%)
    pallas_call x1, Pallas kernels, local(): pl.pallas_call(functools.partial(route_kernel, n_rep, float(rows * n * n_...  34.7 us
    pallas_call x1, Pallas kernels, local(): pl.pallas_call(write_kernel, out_shape=(jax.ShapeDtypeStruct((slots, widt...  1.23 us

profile of v3, /device:TPU:1, one launch (start us, length us, event | category | flops | bytes accessed | tf_op | source)
XLA Modules:
  0.0 36.6 jit_solution(2542090471304375631)
XLA Ops:
  0.6 34.7 %route.1 = (f32[3072,128]{1,0:T(8,128)S(1)}, f32[1,384]{1,0:T(1,128)S(1)}, s32[1,128]{1,0:T(1,128)S(1)}) custom-call(bf16[256,1024]{1,0:T(8,128)(2,1)} %bitcast.7, f32[1,256]{1,0:T(1,128)} %bitcast.9, s32[1,128]{1,0:T(1,128)} %bitcast.10, s32[1,128]{1,0:T(1,128)} %bitcast.11, f32[1,1024]{1,0:T(1,128)} %bitcast.8), custom_call_target="tpu_custom_call" | custom-call | tf_op jit(solution)/shard_map/route/pallas_call | solution.py:257
  35.4 1.2 %write.1 = (bf16[384,1024]{1,0:T(8,128)(2,1)}, f32[1,384]{1,0:T(1,128)}, s32[1]{0:T(128)}) custom-call(f32[3072,128]{1,0:T(8,128)S(1)} %get-tuple-element.9.spread_rows, f32[1,384]{1,0:T(1,128)S(1)} %get-tuple-element.10.spread_rews, s32[1,128]{1,0:T(1,128)S(1)} %get-tuple-element.11.count), custom_call_target="tpu_custom_call" | custom-call | tf_op jit(solution)/shard_map/write/pallas_call | solution.py:305

commit v4 on v3

--- a/solution.py
+++ b/solution.py
@@ -13,8 +13,9 @@
 LANES = 128
 SIDE = 8
 FIELDS = 8
-ORDER = (0, 4, 5, 3, 6, 2, 7, 1)
-GROUPS = ((0, 4), (4, 4))
+Z_ORDER = (0, 1, 2, 3, 4, 5, 6, 7)
+Y_ORDER = (0, 1, 2, 3, 7, 6, 5, 4)
+STEPS = (('y', (0, 8), (0, 8)), ('z', (0, 8), (0, 8)))
 VMEM = pl.BlockSpec(memory_space=pltpu.VMEM)
 SMEM = pl.BlockSpec(memory_space=pltpu.SMEM)
 HBM = pl.BlockSpec(memory_space=pltpu.HBM)
@@ -28,13 +29,6 @@
 
 def actor(y, z, c):
     return (lax.rem(y, SIDE) * SIDE + lax.rem(z, SIDE)) * 2 + lax.rem(c, 2)
-
-
-def distance(k):
-    out = jnp.zeros_like(k)
-    for i, d in enumerate(ORDER):
-        out = jnp.where(k == i, d, out)
-    return out
 
 
 def wait(sem, ref):
@@ -64,7 +58,7 @@
     for copy in inputs:
         copy.start()
     barrier = pltpu.get_barrier_semaphore()
-    for d in ORDER[1:]:
+    for d in range(1, SIDE):
         for peer in (actor(y, z + d, c), actor(y + d, z, c), actor(y, z + d, c + 1)):
             pl.semaphore_signal(barrier, inc=1, device_id={"actors": peer}, device_id_type=MESH)
     pl.semaphore_signal(barrier, inc=1, device_id={"actors": actor(y, z, c + 1)}, device_id_type=MESH)
@@ -75,10 +69,10 @@
 
     row = lax.broadcasted_iota(jnp.int32, (games, 1), 0)
     inner = row & (SIDE - 1)
-    step = distance((row // SIDE) & (SIDE - 1))
+    step = (row // SIDE) & (SIDE - 1)
     near = row < games // 2
-    to_y = jnp.where(near, inner, (y + step) & (SIDE - 1))
-    to_z = jnp.where(near, (z + step) & (SIDE - 1), inner)
+    to_y = jnp.where(near, inner, step)
+    to_z = jnp.where(near, step, inner)
     trainer = (to_y * SIDE + to_z) * 2 + jnp.where(near, c, 1 - c)
     length = lens[...].astype(jnp.float32)
     game = lax.broadcasted_iota(jnp.int32, (games, games), 1).astype(jnp.float32)
@@ -120,9 +114,9 @@
                     t * 8 : t * 8 + 8, q * LANES : (q + 1) * LANES
                 ]
     packed[...] = wide[...].astype(jnp.bfloat16).reshape(packed.shape)
-    via_z[0] = packed[0, 0]
-    via_y[0] = packed[1, 0]
-    notes1[0] = note_z[0]
+    via_z[z] = packed[0, z]
+    via_y[y] = packed[1, y]
+    notes1[z] = note_z[z]
 
     pl.semaphore_wait(barrier, 3 * SIDE - 2 + n_rep - 1)
 
@@ -131,42 +125,59 @@
             src_ref=src, dst_ref=dst, send_sem=send_sem, recv_sem=recv_sem, device_id=peer, device_id_type=MESH
         ).start()
 
-    for k in range(SIDE):
-        d = ORDER[k]
-        if k:
-            send(note_z.at[k], notes1.at[k], n1_send, n1_recv, {"actors": actor(y, z + d, c)})
-        send(
-            note_c.at[lax.rem(z + d, SIDE)], notes1.at[SIDE + k], n1_send, n1_recv,
-            {"actors": actor(y, z + d, c + 1)},
-        )
-    for k in range(1, SIDE):
-        d = ORDER[k]
-        send(packed.at[0, k], via_z.at[k], a_send, a_recv.at[k], {"actors": actor(y, z + d, c)})
-        send(packed.at[1, k], via_y.at[k], b_send, b_recv.at[k], {"actors": actor(y + d, z, c)})
+    for k in Z_ORDER:
+
+        @pl.when(k != z)
+        def _():
+            send(note_z.at[k], notes1.at[z], n1_send, n1_recv, {"actors": actor(y, k, c)})
+
+        send(note_c.at[k], notes1.at[SIDE + z], n1_send, n1_recv, {"actors": actor(y, k, c + 1)})
+    for to_z, to_y in zip(Z_ORDER, Y_ORDER):
+
+        @pl.when(to_z != z)
+        def _():
+            send(packed.at[0, to_z], via_z.at[z], a_send, a_recv.at[z], {"actors": actor(y, to_z, c)})
+
+        @pl.when(to_y != y)
+        def _():
+            send(packed.at[1, to_y], via_y.at[y], b_send, b_recv.at[y], {"actors": actor(to_y, z, c)})
 
     wait(n1_recv, notes1.at[pl.ds(1, 2 * SIDE - 1)])
-    notes2[0] = notes1[0:SIDE] + notes1[SIDE:]
-    for k in range(1, SIDE):
-        send(notes2.at[0], notes2.at[k], n2_send, n2_recv, {"actors": actor(y + ORDER[k], z, c)})
-
-    for g, (low, count) in enumerate(GROUPS):
-        some = pl.ds(low, count)
-        for k in range(max(low, 1), low + count):
-            wait(a_recv.at[k], via_z.at[k])
-        for k in range(1, SIDE):
-            d = ORDER[k]
-            send(
-                via_z.at[some, lax.rem(y + d, SIDE)], land_z.at[k, some], a2_send, a2_recv.at[k, g],
-                {"actors": actor(y + d, z, c)},
-            )
-        for k in range(max(low, 1), low + count):
-            wait(b_recv.at[k], via_y.at[k])
-        for k in range(SIDE):
-            d = ORDER[k]
-            send(
-                via_y.at[some, lax.rem(z + d, SIDE)], land_y.at[k, some], b2_send, b2_recv.at[k, g],
-                {"actors": actor(y, z + d, c + 1)},
-            )
+    notes2[y] = notes1[0:SIDE] + notes1[SIDE:]
+    for k in Y_ORDER:
+
+        @pl.when(k != y)
+        def _():
+            send(notes2.at[y], notes2.at[y], n2_send, n2_recv, {"actors": actor(k, z, c)})
+
+    here = {"y": 0, "z": 0}
+    for at, (axis, (low, high), (first, last)) in enumerate(STEPS):
+        via, arrived_at, mine_at = (via_z, a_recv, z) if axis == "y" else (via_y, b_recv, y)
+        for k in range(here[axis], high):
+
+            @pl.when(k != mine_at)
+            def _():
+                wait(arrived_at.at[k], via.at[k])
+
+        here[axis] = max(here[axis], high)
+        some = pl.ds(low, high - low)
+        for k in Y_ORDER if axis == "y" else Z_ORDER:
+            if not first <= k < last:
+                continue
+            if axis == "y":
+
+                @pl.when(k != y)
+                def _():
+                    send(
+                        via_z.at[some, k], land_z.at[y, some], a2_send, a2_recv.at[y, at],
+                        {"actors": actor(k, z, c)},
+                    )
+
+            else:
+                send(
+                    via_y.at[some, k], land_y.at[z, some], b2_send, b2_recv.at[z, at],
+                    {"actors": actor(y, k, c + 1)},
+                )
 
     wait(n2_recv, notes2.at[pl.ds(1, SIDE - 1)])
     arrived = notes2[...].reshape(SIDE * SIDE, LANES)
@@ -175,12 +186,12 @@
     for k in range(1, n_rep):
         send(mine, others.at[k - 1], s_send.at[k - 1], s_recv.at[k - 1], {"rep": lax.rem(rep + k, n_rep)})
 
-    def widen(value, ky, kz, core):
-        source = actor(y + SIDE - ORDER[ky], z + SIDE - ORDER[kz], core)
+    def widen(value, from_y, from_z, core):
+        source = actor(from_y, from_z, core)
         spread_rows[pl.ds(pl.multiple_of(source * piece, 8), piece), :] = value.astype(jnp.float32)
 
     for k in range(SIDE):
-        widen(via_z[k, y], 0, k, c)
+        widen(via_z[k, y], y, k, c)
 
     for k in range(1, n_rep):
         wait(s_recv.at[k - 1], others.at[k - 1])
@@ -195,8 +206,6 @@
     mean = field(CAP + 1) / row_total
     spread = lax.rsqrt(field(CAP + 2) / row_total - mean * mean + EPS_VAR)
     pair = lax.broadcasted_iota(jnp.int32, (SIDE * SIDE, 1), 0)
-    from_y = (y + SIDE - distance(pair // SIDE)) & (SIDE - 1)
-    from_z = (z + SIDE - distance(pair & (SIDE - 1))) & (SIDE - 1)
     slots = games * CAP
     lane = lax.broadcasted_iota(jnp.int32, (SIDE * SIDE, LANES), 1) - y * FIELDS
 
@@ -205,7 +214,7 @@
 
     out = jnp.zeros((SIDE * SIDE, slots), jnp.float32)
     for h in range(2):
-        source = (from_y * SIDE + from_z) * 2 + jnp.where(h == c, 0, 1)
+        source = pair * 2 + jnp.where(h == c, 0, 1)
         slot = lax.broadcasted_iota(jnp.int32, (SIDE * SIDE, slots), 1) - CAP * source
         held_len = column(h * half + CAP)
         for j in range(CAP):
@@ -213,16 +222,25 @@
             out = out + jnp.where(slot == j, value, 0.0)
     spread_rews[...] = jnp.sum(out, axis=0, keepdims=True)
 
-    for g, (low, count) in enumerate(GROUPS):
-        some = pl.ds(low, count)
-        for k in range(SIDE):
-            if k:
-                wait(a2_recv.at[k, g], land_z.at[k, some])
-                for i in range(low, low + count):
-                    widen(land_z[k, i], k, i, c)
-            wait(b2_recv.at[k, g], land_y.at[k, some])
-            for i in range(low, low + count):
-                widen(land_y[k, i], i, k, c + 1)
+    for at, (axis, (low, high), (first, last)) in enumerate(STEPS):
+        some = pl.ds(low, high - low)
+        mine_at = y if axis == "y" else z
+
+        @pl.when((mine_at >= first) & (mine_at < last))
+        def _():
+            for k in Y_ORDER if axis == "y" else Z_ORDER:
+                if axis == "y":
+
+                    @pl.when(k != y)
+                    def _():
+                        wait(a2_recv.at[k, at], land_z.at[k, some])
+                        for i in range(low, high):
+                            widen(land_z[k, i], k, i, c)
+
+                else:
+                    wait(b2_recv.at[k, at], land_y.at[k, some])
+                    for i in range(low, high):
+                        widen(land_y[k, i], i, k, c + 1)
 
     rest = pl.ds(1, SIDE - 1)
     wait(n1_send, notes1.at[pl.ds(1, 2 * SIDE - 1)])
@@ -288,8 +306,8 @@
             DMA((SIDE,)),
             DMA,
             DMA,
-            DMA((SIDE, len(GROUPS))),
-            DMA((SIDE, len(GROUPS))),
+            DMA((SIDE, len(STEPS))),
+            DMA((SIDE, len(STEPS))),
             DMA,
             DMA,
             DMA,

time: 36.7 us -> 35.5 us (0.967)
  the two profiles are of different devices: /device:TPU:1 before, /device:TPU:144 now
where the time goes in v4:
time: 35.5 us; the launch traced here: 35.4 us
  Pallas kernels  34.7 us (98%)
  between operations  0.64 us (2%)
    pallas_call x1, Pallas kernels, local(): pl.pallas_call(functools.partial(route_kernel, n_rep, float(rows * n * n_...  33.5 us
    pallas_call x1, Pallas kernels, local(): pl.pallas_call(write_kernel, out_shape=(jax.ShapeDtypeStruct((slots, widt...  1.23 us

profile of v4, /device:TPU:144, one launch (start us, length us, event | category | flops | bytes accessed | tf_op | source)
XLA Modules:
  0.0 35.4 jit_solution(3889410146523083440)
XLA Ops:
  0.6 33.5 %route.1 = (f32[3072,128]{1,0:T(8,128)S(1)}, f32[1,384]{1,0:T(1,128)S(1)}, s32[1,128]{1,0:T(1,128)S(1)}) custom-call(bf16[256,1024]{1,0:T(8,128)(2,1)} %bitcast.7, f32[1,256]{1,0:T(1,128)} %bitcast.9, s32[1,128]{1,0:T(1,128)} %bitcast.10, s32[1,128]{1,0:T(1,128)} %bitcast.11, f32[1,1024]{1,0:T(1,128)} %bitcast.8), custom_call_target="tpu_custom_call" | custom-call | tf_op jit(solution)/shard_map/route/pallas_call | solution.py:275
  34.1 1.2 %write.1 = (bf16[384,1024]{1,0:T(8,128)(2,1)}, f32[1,384]{1,0:T(1,128)}, s32[1]{0:T(128)}) custom-call(f32[3072,128]{1,0:T(8,128)S(1)} %get-tuple-element.9.spread_rows, f32[1,384]{1,0:T(1,128)S(1)} %get-tuple-element.10.spread_rews, s32[1,128]{1,0:T(1,128)S(1)} %get-tuple-element.11.count), custom_call_target="tpu_custom_call" | custom-call | tf_op jit(solution)/shard_map/write/pallas_call | solution.py:323

commit v5 on v4

--- a/solution.py
+++ b/solution.py
@@ -55,15 +55,15 @@
             ((feats_in, feats), (rews_in, rews), (lens_in, lens), (owns_in, owns), (gain_in, gain))
         )
     ]
-    for copy in inputs:
-        copy.start()
     barrier = pltpu.get_barrier_semaphore()
-    for d in range(1, SIDE):
+    for d in (4, 5, 3, 6, 2, 7, 1):
         for peer in (actor(y, z + d, c), actor(y + d, z, c), actor(y, z + d, c + 1)):
             pl.semaphore_signal(barrier, inc=1, device_id={"actors": peer}, device_id_type=MESH)
     pl.semaphore_signal(barrier, inc=1, device_id={"actors": actor(y, z, c + 1)}, device_id_type=MESH)
     for k in range(1, n_rep):
         pl.semaphore_signal(barrier, inc=1, device_id={"rep": lax.rem(rep + k, n_rep)}, device_id_type=MESH)
+    for copy in inputs:
+        copy.start()
     for copy in inputs[1:]:
         copy.wait()
 

time: 35.5 us -> 35.5 us (level)
  no operation moved by 1% of the time
where the time goes in v5:
time: 35.5 us; the launch traced here: 35.4 us
  Pallas kernels  34.7 us (98%)
  between operations  0.64 us (2%)
    pallas_call x1, Pallas kernels, local(): pl.pallas_call(functools.partial(route_kernel, n_rep, float(rows * n * n_...  33.5 us
    pallas_call x1, Pallas kernels, local(): pl.pallas_call(write_kernel, out_shape=(jax.ShapeDtypeStruct((slots, widt...  1.23 us

profile of v5, /device:TPU:144, one launch (start us, length us, event | category | flops | bytes accessed | tf_op | source)
XLA Modules:
  0.0 35.4 jit_solution(7300021454297401352)
XLA Ops:
  0.6 33.5 %route.1 = (f32[3072,128]{1,0:T(8,128)S(1)}, f32[1,384]{1,0:T(1,128)S(1)}, s32[1,128]{1,0:T(1,128)S(1)}) custom-call(bf16[256,1024]{1,0:T(8,128)(2,1)} %bitcast.7, f32[1,256]{1,0:T(1,128)} %bitcast.9, s32[1,128]{1,0:T(1,128)} %bitcast.10, s32[1,128]{1,0:T(1,128)} %bitcast.11, f32[1,1024]{1,0:T(1,128)} %bitcast.8), custom_call_target="tpu_custom_call" | custom-call | tf_op jit(solution)/shard_map/route/pallas_call | solution.py:275
  34.1 1.2 %write.1 = (bf16[384,1024]{1,0:T(8,128)(2,1)}, f32[1,384]{1,0:T(1,128)}, s32[1]{0:T(128)}) custom-call(f32[3072,128]{1,0:T(8,128)S(1)} %get-tuple-element.9.spread_rows, f32[1,384]{1,0:T(1,128)S(1)} %get-tuple-element.10.spread_rews, s32[1,128]{1,0:T(1,128)S(1)} %get-tuple-element.11.count), custom_call_target="tpu_custom_call" | custom-call | tf_op jit(solution)/shard_map/write/pallas_call | solution.py:323

commit v6 on v5

--- a/solution.py
+++ b/solution.py
@@ -29,6 +29,11 @@
 
 def actor(y, z, c):
     return (lax.rem(y, SIDE) * SIDE + lax.rem(z, SIDE)) * 2 + lax.rem(c, 2)
+
+
+def y_turns(y):
+    half = SIDE // 2
+    return [part + lax.rem(y + i, half) for part in (0, half) for i in range(half)]
 
 
 def wait(sem, ref):
@@ -125,14 +130,14 @@
             src_ref=src, dst_ref=dst, send_sem=send_sem, recv_sem=recv_sem, device_id=peer, device_id_type=MESH
         ).start()
 
-    for k in Z_ORDER:
+    for k in Z_ORDER[::-1]:
 
         @pl.when(k != z)
         def _():
             send(note_z.at[k], notes1.at[z], n1_send, n1_recv, {"actors": actor(y, k, c)})
 
         send(note_c.at[k], notes1.at[SIDE + z], n1_send, n1_recv, {"actors": actor(y, k, c + 1)})
-    for to_z, to_y in zip(Z_ORDER, Y_ORDER):
+    for to_z, to_y in zip(Z_ORDER, y_turns(y)):
 
         @pl.when(to_z != z)
         def _():
@@ -161,9 +166,7 @@
 
         here[axis] = max(here[axis], high)
         some = pl.ds(low, high - low)
-        for k in Y_ORDER if axis == "y" else Z_ORDER:
-            if not first <= k < last:
-                continue
+        for k in y_turns(y) if axis == "y" else Z_ORDER:
             if axis == "y":
 
                 @pl.when(k != y)

time: 35.5 us -> 35.5 us (level)
  no operation moved by 1% of the time
where the time goes in v6:
time: 35.5 us; the launch traced here: 35.3 us
  Pallas kernels  34.7 us (98%)
  between operations  0.64 us (2%)
    pallas_call x1, Pallas kernels, local(): pl.pallas_call(functools.partial(route_kernel, n_rep, float(rows * n * n_...  33.5 us
    pallas_call x1, Pallas kernels, local(): pl.pallas_call(write_kernel, out_shape=(jax.ShapeDtypeStruct((slots, widt...  1.23 us

profile of v6, /device:TPU:144, one launch (start us, length us, event | category | flops | bytes accessed | tf_op | source)
XLA Modules:
  0.0 35.3 jit_solution(13174202206613454735)
XLA Ops:
  0.6 33.5 %route.1 = (f32[3072,128]{1,0:T(8,128)S(1)}, f32[1,384]{1,0:T(1,128)S(1)}, s32[1,128]{1,0:T(1,128)S(1)}) custom-call(bf16[256,1024]{1,0:T(8,128)(2,1)} %bitcast.7, f32[1,256]{1,0:T(1,128)} %bitcast.9, s32[1,128]{1,0:T(1,128)} %bitcast.10, s32[1,128]{1,0:T(1,128)} %bitcast.11, f32[1,1024]{1,0:T(1,128)} %bitcast.8), custom_call_target="tpu_custom_call" | custom-call | tf_op jit(solution)/shard_map/route/pallas_call | solution.py:278
  34.1 1.2 %write.1 = (bf16[384,1024]{1,0:T(8,128)(2,1)}, f32[1,384]{1,0:T(1,128)}, s32[1]{0:T(128)}) custom-call(f32[3072,128]{1,0:T(8,128)S(1)} %get-tuple-element.9.spread_rows, f32[1,384]{1,0:T(1,128)S(1)} %get-tuple-element.10.spread_rews, s32[1,128]{1,0:T(1,128)S(1)} %get-tuple-element.11.count), custom_call_target="tpu_custom_call" | custom-call | tf_op jit(solution)/shard_map/write/pallas_call | solution.py:326
